TPU v7x, 32 devices: a whole 2x2x4 slice. The times are simulated.
32 devices in a mesh: rep: 4 (over z), inst: 8 (over y, x, core).
Axes of the slice: x: 2, y: 2, z: 4, core: 2. Of those that a mesh axis runs over, the one named last changes fastest.
Arguments:
- acts: bfloat16 [32768, 4096], P(('rep', 'inst')), may hold values from -6 to 6
- grad_keys: bfloat16 [32768, 1024], P(('rep', 'inst')), may hold values from -0.0625 to 0.0625
- grad_values: bfloat16 [32768, 1024], P(('rep', 'inst')), may hold values from -0.0625 to 0.0625
- grad_logits: bfloat16 [8, 32768], P(None, ('rep', 'inst')), may hold values from -0.0625 to 0.0625
- order: int32 [32], replicated, may hold values from 0 to 31, each once
- bucket_param: float32 [4, 2048, 1024], P(None, 'inst'), may hold values from -6 to 6
- bucket_m: float32 [4, 2048, 1024], P(None, 'inst'), may hold values from -6 to 6
- bucket_v: float32 [4, 2048, 1024], P(None, 'inst'), may hold values from 0.25 to 4
- router_param: float32 [32, 1024], P('inst'), may hold values from -6 to 6
- router_m: float32 [32, 1024], P('inst'), may hold values from -6 to 6
- router_v: float32 [32, 1024], P('inst'), may hold values from 0.25 to 4
Outputs:
- new_param: float32 [4, 2048, 1024], P(None, 'inst')
- new_moment: float32 [4, 2048, 1024], P(None, 'inst')
- new_second: float32 [4, 2048, 1024], P(None, 'inst')
- router_new_param: float32 [32, 1024], P('inst')
- router_new_moment: float32 [32, 1024], P('inst')
- router_new_second: float32 [32, 1024], P('inst')
Inputs may be any that keep to these rules, and one draw needn't show every extreme that they name: order is a permutation of the 32 row blocks; entries with k * 8 <= s < (k + 1) * 8 fill bucket k.
All inputs are finite; a program needn't handle non-finite values.
Results may differ from a plain program's by a relative error of at most 0.0003.
Values sent between devices are 32-bit elements; how exact they have to be, the bound alone decides.
A program may use at most 256 MiB of HBM per device.

v0:
```python
import jax
import jax.numpy as jnp
from jax import lax
from jax.sharding import PartitionSpec as P

BUCKETS = 4
BLOCK_ROWS = 256
beta_first = 0.9
beta_second = 0.95
step_rate = 0.05
decay_rate = 0.1
epsilon = 1e-08
correct_first = 1.0 - 0.9**10
correct_second = 1.0 - 0.95**10


def contract(left, right):
    return lax.dot_general(
        left, right, (((0,), (0,)), ((), ())), preferred_element_type=jnp.float32
    )


def adamw(grad, param, moment, second):
    moment_new = beta_first * moment + (1.0 - beta_first) * grad
    second_new = beta_second * second + (1.0 - beta_second) * grad * grad
    ratio = moment_new / correct_first / (jnp.sqrt(second_new / correct_second) + epsilon)
    param_new = param - step_rate * (ratio + decay_rate * param)
    return (param_new, moment_new, second_new)


def owner_step(term, param, moment, second):
    share = lax.psum_scatter(term, "inst", scatter_dimension=0, tiled=True)
    total = lax.psum(share, "rep")
    return adamw(total, param, moment, second)


def on_device(
    acts,
    grad_keys,
    grad_values,
    grad_logits,
    order,
    bucket_param,
    bucket_m,
    bucket_v,
    router_param,
    router_m,
    router_v,
):
    per_bucket = order.shape[0] // BUCKETS
    weight_rows = jnp.concatenate([contract(acts, grad_keys), contract(acts, grad_values)], axis=0)
    params_out = []
    moments_out = []
    seconds_out = []
    for bucket in range(BUCKETS):
        pieces = []
        for slot in range(per_bucket):
            block = order[bucket * per_bucket + slot]
            pieces.append(lax.dynamic_slice_in_dim(weight_rows, block * BLOCK_ROWS, BLOCK_ROWS, 0))
        term = jnp.concatenate(pieces, axis=0)
        fresh = owner_step(term, bucket_param[bucket], bucket_m[bucket], bucket_v[bucket])
        params_out.append(fresh[0])
        moments_out.append(fresh[1])
        seconds_out.append(fresh[2])
    router_term = jnp.dot(grad_logits, acts, preferred_element_type=jnp.float32)
    router_term = router_term.reshape(-1, router_param.shape[1])
    router_share = lax.psum_scatter(router_term, "inst", scatter_dimension=0, tiled=True)
    router_total = lax.psum(router_share, "rep")
    router_fresh = adamw(router_total, router_param, router_m, router_v)
    return (
        jnp.stack(params_out),
        jnp.stack(moments_out),
        jnp.stack(seconds_out),
        router_fresh[0],
        router_fresh[1],
        router_fresh[2],
    )


def solution(mesh):
    return jax.shard_map(
        on_device,
        mesh=mesh,
        in_specs=(
            P(("rep", "inst"), None),
            P(("rep", "inst"), None),
            P(("rep", "inst"), None),
            P(None, ("rep", "inst")),
            P(),
            P(None, "inst", None),
            P(None, "inst", None),
            P(None, "inst", None),
            P("inst", None),
            P("inst", None),
            P("inst", None),
        ),
        out_specs=(
            P(None, "inst", None),
            P(None, "inst", None),
            P(None, "inst", None),
            P("inst", None),
            P("inst", None),
            P("inst", None),
        ),
        check_vma=False,
    )
```

profile of v0, /device:TPU:0, one launch (start us, length us, event | category | flops | bytes accessed | tf_op | source)
XLA Modules:
  0.0 603.0 jit_solution(1667637888820862590)
XLA Ops:
  7.2 1.8 fusion.91
  14.1 2.1 fusion.90
  18.2 14.8 %fusion.92 = f32[4096,1024]{1,0:T(8,128)} fusion(bf16[1024,4096]{1,0:T(8,128)(2,1)} %param.11, bf16[1024,1024]{1,0:T(8,128)(2,1)S(1)} %copy-done), kind=kOutput, calls=%fused_computation.178 | convolution fusion | flops 8589934592 | bytes 27262976 | tf_op jit(solution)/shard_map/dot_general | solution.py:18
  33.0 11.5 %fusion.93 = f32[4096,1024]{1,0:T(8,128)} fusion(bf16[1024,4096]{1,0:T(8,128)(2,1)S(1)} %copy-done.4, bf16[1024,1024]{1,0:T(8,128)(2,1)S(1)} %copy-done.16), kind=kOutput, calls=%fused_computation.179 | convolution fusion | flops 8589934592 | bytes 27262976 | tf_op jit(solution)/shard_map/dot_general | solution.py:18
  44.6 1.6 fusion.3
  46.2 4.4 copy-done.2
  50.6 4.8 copy-done.3
  57.1 4.1 fusion.17
  61.3 3.3 copy-done.6
  70.6 2.7 fusion.21
  73.4 3.4 fusion.23
  78.0 1.9 slice-done.13
  80.0 2.1 slice-done.2
  82.0 1.8 slice-done.3
  91.6 2.4 fusion.33
  98.5 2.8 fusion.39
  101.3 3.6 fusion.41
  105.0 1.5 slice-done.17
  115.5 2.1 fusion.49
  120.8 2.7 fusion.57
  123.6 3.8 fusion.59
  138.1 4.6 fusion.94
  143.6 70.3 %reduce-scatter.7.cloned.1.call-done = f32[256,1024]{1,0:T(8,128)} async-done(((f32[2048,1024]{1,0:T(8,128)}), f32[256,1024]{1,0:T(8,128)}) %reduce-scatter.7.cloned.1.call-update) | async-done | bytes 1048592 | tf_op jit(solution)/shard_map/reduce_scatter | solution.py:32
  213.9 75.0 %reduce-scatter.9.cloned.1.call-done = f32[256,1024]{1,0:T(8,128)} async-done(((f32[2048,1024]{1,0:T(8,128)}), f32[256,1024]{1,0:T(8,128)}) %reduce-scatter.9.cloned.1.call-update) | async-done | bytes 1048592 | tf_op jit(solution)/shard_map/reduce_scatter | solution.py:32
  288.9 74.8 %reduce-scatter.11.cloned.1.call-done = f32[256,1024]{1,0:T(8,128)} async-done(((f32[2048,1024]{1,0:T(8,128)}), f32[256,1024]{1,0:T(8,128)}) %reduce-scatter.11.cloned.1.call-update) | async-done | bytes 1048592 | tf_op jit(solution)/shard_map/reduce_scatter | solution.py:32
  365.0 55.6 %all-reduce.5.cloned.1.call-done = f32[32,1024]{1,0:T(8,128)} async-done(((f32[32,1024]{1,0:T(8,128)}), f32[32,1024]{1,0:T(8,128)}) %all-reduce.5.cloned.1.call-update) | async-done | bytes 131088
  421.4 19.5 %psum.39 = f32[4,1024]{1,0:T(4,128)S(1)} all-reduce(f32[4,1024]{1,0:T(4,128)S(1)} %constant_dynamic-slice_fusion), channel_id=1, replica_groups=mesh['rep'=4,'inst'=8] {'rep'}, use_global_device_ids=true, to_apply=%region_9.0 | all-reduce | flops 4096 | bytes 32768 | tf_op jit(solution)/shard_map/psum | solution.py:68
  441.6 136.1 %all-reduce.7.cloned.1.call-done = (f32[256,1024]{1,0:T(8,128)}, f32[256,1024]{1,0:T(8,128)}, f32[256,1024]{1,0:T(8,128)}, f32[256,1024]{1,0:T(8,128)}) async-done(((f32[256,1024]{1,0:T(8,128)}, f32[256,1024]{1,0:T(8,128)}, f32[256,1024]{1,0:T(8,128)}, f32[256,1024]{1,0:T(8,128)}), (f32[256,1024]{1,0:T(8,128)}, f32[256,1024]{1,0:T(8,128)}, f32[256,1024]{1,0:T(8,128)}, ...) | async-done | bytes 4194320 | tf_op jit(solution)/shard_map/psum | solution.py:33
  577.7 5.6 fusion.80
  585.0 4.7 fusion.79
  589.7 2.6 pad_maximum_fusion.1
  592.3 3.8 pad_maximum_fusion
  (116 shorter events, 35.4 us)
Async XLA Ops:
  7.2 11.0 %copy-start = (bf16[1024,1024]{1,0:T(8,128)(2,1)S(1)}, bf16[1024,1024]{1,0:T(8,128)(2,1)}, u32[]{:S(2)}) copy-start(bf16[1024,1024]{1,0:T(8,128)(2,1)} %param.12) | copy-start | bytes 6291460
  7.2 136.4 %reduce-scatter.5.cloned.1.call-start = ((), (), s32[]{:S(2)}) async-start(), calls=%async_computation.4 | async-start | bytes 9437184 | tf_op jit(solution)/shard_map/reduce_scatter | solution.py:32
  18.2 14.8 %copy-start.4 = (bf16[1024,4096]{1,0:T(8,128)(2,1)S(1)}, bf16[1024,4096]{1,0:T(8,128)(2,1)}, u32[]{:S(2)}) copy-start(bf16[1024,4096]{1,0:T(8,128)(2,1)} %param.11) | copy-start | bytes 25165828
  18.2 14.8 %copy-start.16 = (bf16[1024,1024]{1,0:T(8,128)(2,1)S(1)}, bf16[1024,1024]{1,0:T(8,128)(2,1)}, u32[]{:S(2)}) copy-start(bf16[1024,1024]{1,0:T(8,128)(2,1)} %param.13) | copy-start | bytes 6291460
  44.6 10.9 %copy-start.3 = (f32[4096,1024]{1,0:T(8,128)S(1)}, f32[4096,1024]{1,0:T(8,128)}, u32[]{:S(2)}) copy-start(f32[4096,1024]{1,0:T(8,128)} %fusion.93) | copy-start | bytes 50331652
  64.6 149.4 %reduce-scatter.7.cloned.1.call-start = ((), (), s32[]{:S(2)}) async-start(), calls=%async_computation.5 | async-start | bytes 9437184 | tf_op jit(solution)/shard_map/reduce_scatter | solution.py:32
  70.6 7.4 %slice-start.12 = ((s8[16777216]{0:T(1024)(128)(4,1)}), s8[4194304]{0:T(1024)(128)(4,1)S(1)}, s32[]{:S(2)}) async-start(s8[16777216]{0:T(1024)(128)(4,1)} %bitcast.161), calls=%async_computation.22 | async-start | bytes 8388608
  70.6 9.3 %slice-start.13 = ((s8[16777216]{0:T(1024)(128)(4,1)}), s8[4194304]{0:T(1024)(128)(4,1)S(1)}, s32[]{:S(2)}) async-start(s8[16777216]{0:T(1024)(128)(4,1)} %bitcast.161), calls=%async_computation.23 | async-start | bytes 8388608
  73.4 8.6 %slice-start.2 = ((s8[16777216]{0:T(1024)(128)(4,1)}), s8[4194304]{0:T(1024)(128)(4,1)S(1)}, s32[]{:S(2)}) async-start(s8[16777216]{0:T(1024)(128)(4,1)} %bitcast.155), calls=%async_computation.12 | async-start | bytes 8388608
  73.4 10.5 %slice-start.3 = ((s8[16777216]{0:T(1024)(128)(4,1)}), s8[4194304]{0:T(1024)(128)(4,1)S(1)}, s32[]{:S(2)}) async-start(s8[16777216]{0:T(1024)(128)(4,1)} %bitcast.155), calls=%async_computation.13 | async-start | bytes 8388608
  73.4 11.8 %slice-start.14 = ((s8[16777216]{0:T(1024)(128)(4,1)}), s8[4194304]{0:T(1024)(128)(4,1)S(1)}, s32[]{:S(2)}) async-start(s8[16777216]{0:T(1024)(128)(4,1)} %bitcast.161), calls=%async_computation.24 | async-start | bytes 8388608
  73.4 13.2 %slice-start.15 = ((s8[16777216]{0:T(1024)(128)(4,1)}), s8[4194304]{0:T(1024)(128)(4,1)S(1)}, s32[]{:S(2)}) async-start(s8[16777216]{0:T(1024)(128)(4,1)} %bitcast.161), calls=%async_computation.25 | async-start | bytes 8388608
  94.0 194.9 %reduce-scatter.9.cloned.1.call-start = ((), (), s32[]{:S(2)}) async-start(), calls=%async_computation.6 | async-start | bytes 9437184 | tf_op jit(solution)/shard_map/reduce_scatter | solution.py:32
  98.5 8.0 %slice-start.17 = ((s8[16777216]{0:T(1024)(128)(4,1)}), s8[4194304]{0:T(1024)(128)(4,1)S(1)}, s32[]{:S(2)}) async-start(s8[16777216]{0:T(1024)(128)(4,1)} %bitcast.163), calls=%async_computation.27 | async-start | bytes 8388608
  101.3 7.9 %slice-start.7 = ((s8[16777216]{0:T(1024)(128)(4,1)}), s8[4194304]{0:T(1024)(128)(4,1)S(1)}, s32[]{:S(2)}) async-start(s8[16777216]{0:T(1024)(128)(4,1)} %bitcast.157), calls=%async_computation.17 | async-start | bytes 8388608
  101.3 9.1 %slice-start.18 = ((s8[16777216]{0:T(1024)(128)(4,1)}), s8[4194304]{0:T(1024)(128)(4,1)S(1)}, s32[]{:S(2)}) async-start(s8[16777216]{0:T(1024)(128)(4,1)} %bitcast.163), calls=%async_computation.28 | async-start | bytes 8388608
  101.3 10.4 %slice-start.19 = ((s8[16777216]{0:T(1024)(128)(4,1)}), s8[4194304]{0:T(1024)(128)(4,1)S(1)}, s32[]{:S(2)}) async-start(s8[16777216]{0:T(1024)(128)(4,1)} %bitcast.163), calls=%async_computation.29 | async-start | bytes 8388608
  117.7 246.1 %reduce-scatter.11.cloned.1.call-start = ((), (), s32[]{:S(2)}) async-start(), calls=%async_computation.7 | async-start | bytes 9437184 | tf_op jit(solution)/shard_map/reduce_scatter | solution.py:32
  120.8 6.6 %slice-start.8 = ((s8[16777216]{0:T(1024)(128)(4,1)}), s8[4194304]{0:T(1024)(128)(4,1)S(1)}, s32[]{:S(2)}) async-start(s8[16777216]{0:T(1024)(128)(4,1)} %bitcast.159), calls=%async_computation.18 | async-start | bytes 8388608
  120.8 7.9 %slice-start.21 = ((s8[16777216]{0:T(1024)(128)(4,1)}), s8[4194304]{0:T(1024)(128)(4,1)S(1)}, s32[]{:S(2)}) async-start(s8[16777216]{0:T(1024)(128)(4,1)} %bitcast.165), calls=%async_computation.31 | async-start | bytes 8388608
  123.6 7.6 %slice-start.11 = ((s8[16777216]{0:T(1024)(128)(4,1)}), s8[4194304]{0:T(1024)(128)(4,1)S(1)}, s32[]{:S(2)}) async-start(s8[16777216]{0:T(1024)(128)(4,1)} %bitcast.159), calls=%async_computation.21 | async-start | bytes 8388608
  123.6 8.8 %slice-start.22 = ((s8[16777216]{0:T(1024)(128)(4,1)}), s8[4194304]{0:T(1024)(128)(4,1)S(1)}, s32[]{:S(2)}) async-start(s8[16777216]{0:T(1024)(128)(4,1)} %bitcast.165), calls=%async_computation.32 | async-start | bytes 8388608
  123.6 10.0 %slice-start.23 = ((s8[16777216]{0:T(1024)(128)(4,1)}), s8[4194304]{0:T(1024)(128)(4,1)S(1)}, s32[]{:S(2)}) async-start(s8[16777216]{0:T(1024)(128)(4,1)} %bitcast.165), calls=%async_computation.33 | async-start | bytes 8388608
  137.4 226.3 %copy-start.17 = (u32[32]{0:T(128)S(1)}, u32[32]{0:T(128)}, u32[]{:S(2)}) copy-start(u32[32]{0:T(128)} %constant.74) | copy-start | bytes 388
  137.5 303.5 %copy-start.13 = (f32[4,1024]{1,0:T(4,128)S(1)}, f32[4,1024]{1,0:T(4,128)}, u32[]{:S(2)}) copy-start(f32[4,1024]{1,0:T(4,128)} %param.19) | copy-start | bytes 49156
  137.5 303.5 %copy-start.14 = (f32[4,1024]{1,0:T(4,128)S(1)}, f32[4,1024]{1,0:T(4,128)}, u32[]{:S(2)}) copy-start(f32[4,1024]{1,0:T(4,128)} %param.20) | copy-start | bytes 49156
  137.5 303.5 %copy-start.15 = (f32[4,1024]{1,0:T(4,128)S(1)}, f32[4,1024]{1,0:T(4,128)}, u32[]{:S(2)}) copy-start(f32[4,1024]{1,0:T(4,128)} %param.21) | copy-start | bytes 49156
  137.5 283.2 %all-reduce.5.cloned.1.call-start = ((), (), s32[]{:S(2)}) async-start(), calls=%async_computation.8 | async-start | bytes 262144
  143.5 434.2 %all-reduce.7.cloned.1.call-start = ((), (), s32[]{:S(2)}) async-start(), calls=%async_computation.9 | async-start | bytes 8388608 | tf_op jit(solution)/shard_map/psum | solution.py:33
  577.7 6.7 %copy-start.9 = (f32[256,1024]{1,0:T(8,128)S(1)}, f32[256,1024]{1,0:T(8,128)}, u32[]{:S(2)}) copy-start(f32[256,1024]{1,0:T(8,128)} %get-tuple-element.7) | copy-start | bytes 3145732
  577.7 7.0 %copy-start.10 = (f32[256,1024]{1,0:T(8,128)S(1)}, f32[256,1024]{1,0:T(8,128)}, u32[]{:S(2)}) copy-start(f32[256,1024]{1,0:T(8,128)} %get-tuple-element.8) | copy-start | bytes 3145732
  577.7 7.3 %copy-start.11 = (f32[256,1024]{1,0:T(8,128)S(1)}, f32[256,1024]{1,0:T(8,128)}, u32[]{:S(2)}) copy-start(f32[256,1024]{1,0:T(8,128)} %get-tuple-element.9) | copy-start | bytes 3145732
  (16 other events, 90.2 us)
Sparse Core Ops, SparseCore 0:
  64.7 74.2 reduce-scatter.4
  142.4 71.4 reduce-scatter.6
  217.4 71.4 reduce-scatter.8
  292.2 71.4 reduce-scatter.10
  367.2 53.3 all-reduce.4
  423.1 154.5 all-reduce.6
where the time goes:
time: 604 us; the launch traced here: 603 us
  waiting for transfers between devices  412 us (68%)
  other arithmetic  61.2 us (10%)
  local copies, waits for them, and re-layouts  43.5 us (7%)
  between operations  35.4 us (6%)
  matrix products  31 us (5%)
  blocking collectives  19.5 us (3%)
    reduce_scatter x4, waiting for transfers between devices, owner_step(): share = lax.psum_scatter(term, 'inst', scatter_dimension=0, tiled=True)  220 us
    psum x1, waiting for transfers between devices, owner_step(): total = lax.psum(share, 'rep')  136 us
    unnamed x7, waiting for transfers between devices  55.7 us
    unnamed x86, local copies, waits for them, and re-layouts  38.9 us
    unnamed x28, other arithmetic  33.9 us
    dot_general x2, matrix products, contract(): lax.dot_general(left, right, (((0,), (0,)), ((), ())), preferred_element_...  26.3 us
    psum x1, blocking collectives, on_device(): router_total = lax.psum(router_share, 'rep')  19.5 us
  transfers between devices with their start and end apart: 6, of which 5 were waited for; matrix products, arithmetic and copies ran while one was open for 7% of the time, Pallas kernels for 0%

commit v1 on v0

--- a/solution.py
+++ b/solution.py
@@ -12,6 +12,11 @@
 epsilon = 1e-08
 correct_first = 1.0 - 0.9**10
 correct_second = 1.0 - 0.95**10
+
+
+def take_the_sums_all(inner_x):
+    heard = lax.all_gather(inner_x, axis_name="rep")
+    return jnp.sum(heard, axis=0)
 
 
 def contract(left, right):
@@ -30,7 +35,7 @@
 
 def owner_step(term, param, moment, second):
     share = lax.psum_scatter(term, "inst", scatter_dimension=0, tiled=True)
-    total = lax.psum(share, "rep")
+    total = take_the_sums_all(share)
     return adamw(total, param, moment, second)
 
 

time: 604 us -> 780 us (1.29)
  waiting for transfers between devices: 412 us -> 582 us
  other arithmetic: 61.2 us -> 80.3 us
  local copies, waits for them, and re-layouts: 43.5 us -> 30.7 us
    all_gather x0 -> x4, waiting for transfers between devices: none -> 295 us  [take_the_sums_all(): heard = lax.all_gather(inner_x, axis_name='rep')]
    psum x1 -> x0, waiting for transfers between devices: 136 us -> none  [owner_step(): total = lax.psum(share, 'rep')]
    unnamed x86 -> x56, local copies, waits for them, and re-layouts: 38.9 us -> 26.1 us
    reduce_sum x0 -> x4, other arithmetic: none -> 11.8 us  [take_the_sums_all(): return jnp.sum(heard, axis=0)]
    reduce_scatter x4, waiting for transfers between devices: 220 us -> 231 us  [owner_step(): share = lax.psum_scatter(term, 'inst', scatter_dimension=0, tiled=True)]
    unnamed x28 -> x26, other arithmetic: 33.9 us -> 43.4 us
    unnamed x7 -> x10, waiting for transfers between devices: 55.7 us -> 56.3 us
  transfers between devices with their start and end apart: 6 -> 9, of which waited for: 5 -> 9; matrix products, arithmetic and copies ran while one was open for 7% -> 6% of each run, Pallas kernels for 0% -> 0%
where the time goes in v1:
time: 780 us; the launch traced here: 779 us
  waiting for transfers between devices  582 us (75%)
  other arithmetic  80.3 us (10%)
  between operations  34.9 us (4%)
  matrix products  30.9 us (4%)
  local copies, waits for them, and re-layouts  30.7 us (4%)
  blocking collectives  19.5 us (2%)
    all_gather x4, waiting for transfers between devices, take_the_sums_all(): heard = lax.all_gather(inner_x, axis_name='rep')  295 us
    reduce_scatter x4, waiting for transfers between devices, owner_step(): share = lax.psum_scatter(term, 'inst', scatter_dimension=0, tiled=True)  231 us
    unnamed x10, waiting for transfers between devices  56.3 us
    unnamed x26, other arithmetic  43.4 us
    dot_general x2, matrix products, contract(): lax.dot_general(left, right, (((0,), (0,)), ((), ())), preferred_element_...  26.3 us
    unnamed x56, local copies, waits for them, and re-layouts  26.1 us
    psum x1, blocking collectives, on_device(): router_total = lax.psum(router_share, 'rep')  19.5 us
  transfers between devices with their start and end apart: 9, of which 9 were waited for; matrix products, arithmetic and copies ran while one was open for 6% of the time, Pallas kernels for 0%

profile of v1, /device:TPU:0, one launch (start us, length us, event | category | flops | bytes accessed | tf_op | source)
XLA Modules:
  0.0 778.9 jit_solution(2265423443850858630)
XLA Ops:
  18.2 14.8 %fusion.84 = f32[4096,1024]{1,0:T(8,128)} fusion(bf16[1024,4096]{1,0:T(8,128)(2,1)} %param.11, bf16[1024,1024]{1,0:T(8,128)(2,1)S(1)} %copy-done), kind=kOutput, calls=%fused_computation.158 | convolution fusion | flops 8589934592 | bytes 27262976 | tf_op jit(solution)/shard_map/dot_general | solution.py:23
  32.9 11.6 %fusion.85 = f32[4096,1024]{1,0:T(8,128)} fusion(bf16[1024,4096]{1,0:T(8,128)(2,1)S(1)} %copy-done.4, bf16[1024,1024]{1,0:T(8,128)(2,1)S(1)} %copy-done.9), kind=kOutput, calls=%fused_computation.159 | convolution fusion | flops 8589934592 | bytes 27262976 | tf_op jit(solution)/shard_map/dot_general | solution.py:23
  44.5 2.7 fusion.3
  47.2 3.7 copy-done.2
  51.0 4.8 copy-done.3
  57.0 2.6 fusion.7
  59.5 2.6 fusion.9
  62.1 2.6 fusion.11
  67.3 2.6 fusion.15
  69.9 5.4 fusion.17
  81.3 2.7 fusion.21
  84.1 3.4 fusion.23
  112.2 2.9 fusion.39
  115.1 3.6 fusion.41
  138.2 4.6 fusion.86
  143.5 6.2 reduce-scatter.5.cloned.1.call-done
  149.8 74.9 %reduce-scatter.7.cloned.1.call-done = f32[256,1024]{1,0:T(8,128)} async-done(((f32[2048,1024]{1,0:T(8,128)}), f32[256,1024]{1,0:T(8,128)}) %reduce-scatter.7.cloned.1.call-update) | async-done | bytes 1048592 | tf_op jit(solution)/shard_map/reduce_scatter | solution.py:37
  224.8 74.9 %reduce-scatter.11.cloned.1.call-done = f32[256,1024]{1,0:T(8,128)} async-done(((f32[2048,1024]{1,0:T(8,128)}), f32[256,1024]{1,0:T(8,128)}) %reduce-scatter.11.cloned.1.call-update) | async-done | bytes 1048592 | tf_op jit(solution)/shard_map/reduce_scatter | solution.py:37
  299.7 74.8 %reduce-scatter.9.cloned.1.call-done = f32[256,1024]{1,0:T(8,128)} async-done(((f32[2048,1024]{1,0:T(8,128)}), f32[256,1024]{1,0:T(8,128)}) %reduce-scatter.9.cloned.1.call-update) | async-done | bytes 1048592 | tf_op jit(solution)/shard_map/reduce_scatter | solution.py:37
  375.8 55.6 %all-reduce.3.cloned.1.call-done = f32[32,1024]{1,0:T(8,128)} async-done(((f32[32,1024]{1,0:T(8,128)}), f32[32,1024]{1,0:T(8,128)}) %all-reduce.3.cloned.1.call-update) | async-done | bytes 131088
  432.2 19.5 %psum.7 = f32[4,1024]{1,0:T(4,128)S(1)} all-reduce(f32[4,1024]{1,0:T(4,128)S(1)} %constant_dynamic-slice_fusion), channel_id=1, replica_groups=mesh['rep'=4,'inst'=8] {'rep'}, use_global_device_ids=true, to_apply=%region_9.0 | all-reduce | flops 4096 | bytes 32768 | tf_op jit(solution)/shard_map/psum | solution.py:73
  452.3 60.8 %all-gather.9.cloned.1.call-done = f32[1024,1024]{1,0:T(8,128)} async-done(((f32[256,1024]{1,0:T(8,128)}), f32[1024,1024]{1,0:T(8,128)}) %all-gather.9.cloned.1.call-update) | async-done | bytes 4194320 | tf_op jit(solution)/shard_map/all_gather | solution.py:18
  513.2 2.7 reduce_sum.44
  515.9 77.9 %all-gather.11.cloned.1.call-done = f32[1024,1024]{1,0:T(8,128)} async-done(((f32[256,1024]{1,0:T(8,128)}), f32[1024,1024]{1,0:T(8,128)}) %all-gather.11.cloned.1.call-update) | async-done | bytes 4194320 | tf_op jit(solution)/shard_map/all_gather | solution.py:18
  593.8 2.7 reduce_sum.46
  596.5 78.1 %all-gather.15.cloned.1.call-done = f32[1024,1024]{1,0:T(8,128)} async-done(((f32[256,1024]{1,0:T(8,128)}), f32[1024,1024]{1,0:T(8,128)}) %all-gather.15.cloned.1.call-update) | async-done | bytes 4194320 | tf_op jit(solution)/shard_map/all_gather | solution.py:18
  674.6 2.7 reduce_sum.50
  677.4 78.1 %all-gather.13.cloned.1.call-done = f32[1024,1024]{1,0:T(8,128)} async-done(((f32[256,1024]{1,0:T(8,128)}), f32[1024,1024]{1,0:T(8,128)}) %all-gather.13.cloned.1.call-update) | async-done | bytes 4194320 | tf_op jit(solution)/shard_map/all_gather | solution.py:18
  755.5 3.7 reduce_sum.48
  759.2 6.7 multiply_subtract_fusion.3
  765.9 2.6 pad_maximum_fusion.2
  768.5 3.9 pad_maximum_fusion
  (96 shorter events, 47.6 us)
Async XLA Ops:
  7.2 11.0 %copy-start = (bf16[1024,1024]{1,0:T(8,128)(2,1)S(1)}, bf16[1024,1024]{1,0:T(8,128)(2,1)}, u32[]{:S(2)}) copy-start(bf16[1024,1024]{1,0:T(8,128)(2,1)} %param.12) | copy-start | bytes 6291460
  7.2 142.5 %reduce-scatter.5.cloned.1.call-start = ((), (), s32[]{:S(2)}) async-start(), calls=%async_computation.4 | async-start | bytes 9437184 | tf_op jit(solution)/shard_map/reduce_scatter | solution.py:37
  18.1 14.8 %copy-start.4 = (bf16[1024,4096]{1,0:T(8,128)(2,1)S(1)}, bf16[1024,4096]{1,0:T(8,128)(2,1)}, u32[]{:S(2)}) copy-start(bf16[1024,4096]{1,0:T(8,128)(2,1)} %param.11) | copy-start | bytes 25165828
  18.2 14.8 %copy-start.9 = (bf16[1024,1024]{1,0:T(8,128)(2,1)S(1)}, bf16[1024,1024]{1,0:T(8,128)(2,1)}, u32[]{:S(2)}) copy-start(bf16[1024,1024]{1,0:T(8,128)(2,1)} %param.13) | copy-start | bytes 6291460
  44.5 6.5 copy-start.2
  44.5 11.2 %copy-start.3 = (f32[4096,1024]{1,0:T(8,128)S(1)}, f32[4096,1024]{1,0:T(8,128)}, u32[]{:S(2)}) copy-start(f32[4096,1024]{1,0:T(8,128)} %fusion.85) | copy-start | bytes 50331652
  75.3 149.4 %reduce-scatter.7.cloned.1.call-start = ((), (), s32[]{:S(2)}) async-start(), calls=%async_computation.5 | async-start | bytes 9437184 | tf_op jit(solution)/shard_map/reduce_scatter | solution.py:37
  81.3 7.4 slice-start.8
  81.3 9.3 %slice-start.9 = ((s8[16777216]{0:T(1024)(128)(4,1)}), s8[4194304]{0:T(1024)(128)(4,1)S(1)}, s32[]{:S(2)}) async-start(s8[16777216]{0:T(1024)(128)(4,1)} %bitcast.75), calls=%async_computation.22 | async-start | bytes 8388608
  84.1 8.6 %slice-start.2 = ((s8[16777216]{0:T(1024)(128)(4,1)}), s8[4194304]{0:T(1024)(128)(4,1)S(1)}, s32[]{:S(2)}) async-start(s8[16777216]{0:T(1024)(128)(4,1)} %bitcast.71), calls=%async_computation.15 | async-start | bytes 8388608
  84.1 10.4 %slice-start.3 = ((s8[16777216]{0:T(1024)(128)(4,1)}), s8[4194304]{0:T(1024)(128)(4,1)S(1)}, s32[]{:S(2)}) async-start(s8[16777216]{0:T(1024)(128)(4,1)} %bitcast.71), calls=%async_computation.16 | async-start | bytes 8388608
  84.1 11.8 %slice-start.10 = ((s8[16777216]{0:T(1024)(128)(4,1)}), s8[4194304]{0:T(1024)(128)(4,1)S(1)}, s32[]{:S(2)}) async-start(s8[16777216]{0:T(1024)(128)(4,1)} %bitcast.75), calls=%async_computation.23 | async-start | bytes 8388608
  84.1 13.1 %slice-start.11 = ((s8[16777216]{0:T(1024)(128)(4,1)}), s8[4194304]{0:T(1024)(128)(4,1)S(1)}, s32[]{:S(2)}) async-start(s8[16777216]{0:T(1024)(128)(4,1)} %bitcast.75), calls=%async_computation.24 | async-start | bytes 8388608
  104.7 195.0 %reduce-scatter.11.cloned.1.call-start = ((), (), s32[]{:S(2)}) async-start(), calls=%async_computation.7 | async-start | bytes 9437184 | tf_op jit(solution)/shard_map/reduce_scatter | solution.py:37
  112.2 6.5 slice-start.4
  112.2 6.5 slice-start.5
  112.2 6.5 slice-start.12
  112.2 7.9 %slice-start.13 = ((s8[16777216]{0:T(1024)(128)(4,1)}), s8[4194304]{0:T(1024)(128)(4,1)S(1)}, s32[]{:S(2)}) async-start(s8[16777216]{0:T(1024)(128)(4,1)} %bitcast.77), calls=%async_computation.26 | async-start | bytes 8388608
  115.1 6.3 slice-start.6
  115.1 7.6 slice-start.7
  115.1 8.8 %slice-start.14 = ((s8[16777216]{0:T(1024)(128)(4,1)}), s8[4194304]{0:T(1024)(128)(4,1)S(1)}, s32[]{:S(2)}) async-start(s8[16777216]{0:T(1024)(128)(4,1)} %bitcast.77), calls=%async_computation.27 | async-start | bytes 8388608
  115.1 10.1 %slice-start.15 = ((s8[16777216]{0:T(1024)(128)(4,1)}), s8[4194304]{0:T(1024)(128)(4,1)S(1)}, s32[]{:S(2)}) async-start(s8[16777216]{0:T(1024)(128)(4,1)} %bitcast.77), calls=%async_computation.28 | async-start | bytes 8388608
  137.5 237.0 %reduce-scatter.9.cloned.1.call-start = ((), (), s32[]{:S(2)}) async-start(), calls=%async_computation.6 | async-start | bytes 9437184 | tf_op jit(solution)/shard_map/reduce_scatter | solution.py:37
  138.1 236.5 %copy-start.10 = (u32[32]{0:T(128)S(1)}, u32[32]{0:T(128)}, u32[]{:S(2)}) copy-start(u32[32]{0:T(128)} %constant.76) | copy-start | bytes 388
  138.1 313.6 %copy-start.6 = (f32[4,1024]{1,0:T(4,128)S(1)}, f32[4,1024]{1,0:T(4,128)}, u32[]{:S(2)}) copy-start(f32[4,1024]{1,0:T(4,128)} %param.19) | copy-start | bytes 49156
  138.1 313.6 %copy-start.7 = (f32[4,1024]{1,0:T(4,128)S(1)}, f32[4,1024]{1,0:T(4,128)}, u32[]{:S(2)}) copy-start(f32[4,1024]{1,0:T(4,128)} %param.20) | copy-start | bytes 49156
  138.1 313.6 %copy-start.8 = (f32[4,1024]{1,0:T(4,128)S(1)}, f32[4,1024]{1,0:T(4,128)}, u32[]{:S(2)}) copy-start(f32[4,1024]{1,0:T(4,128)} %param.21) | copy-start | bytes 49156
  138.1 293.3 %all-reduce.3.cloned.1.call-start = ((), (), s32[]{:S(2)}) async-start(), calls=%async_computation.12 | async-start | bytes 262144
  143.5 369.7 %all-gather.9.cloned.1.call-start = ((), (), s32[]{:S(2)}) async-start(), calls=%async_computation.8 | async-start | bytes 5242880 | tf_op jit(solution)/shard_map/all_gather | solution.py:18
  149.7 444.1 %all-gather.11.cloned.1.call-start = ((), (), s32[]{:S(2)}) async-start(), calls=%async_computation.9 | async-start | bytes 5242880 | tf_op jit(solution)/shard_map/all_gather | solution.py:18
  224.7 449.9 %all-gather.15.cloned.1.call-start = ((), (), s32[]{:S(2)}) async-start(), calls=%async_computation.11 | async-start | bytes 5242880 | tf_op jit(solution)/shard_map/all_gather | solution.py:18
  299.7 455.8 %all-gather.13.cloned.1.call-start = ((), (), s32[]{:S(2)}) async-start(), calls=%async_computation.10 | async-start | bytes 5242880 | tf_op jit(solution)/shard_map/all_gather | solution.py:18
  (4 other events, 17.0 us)
Sparse Core Ops, SparseCore 0:
  75.4 74.2 reduce-scatter.4
  153.2 71.4 reduce-scatter.6
  228.1 71.4 reduce-scatter.10
  303.0 71.4 reduce-scatter.8
  378.0 53.3 all-reduce.2
  432.8 80.2 all-gather.8
  514.7 79.0 all-gather.10
  595.4 79.2 all-gather.14
  676.2 79.2 all-gather.12
